TPU v7x, 512 devices: a whole 4x8x8 slice. The times are simulated.
512 devices in a mesh: ens: 4 (over z_lo), replica: 32 (over y_lo, x, core), model: 4 (over z_hi, y_hi).
Axes of the slice: x: 4, y: 8 (y_hi: 2, y_lo: 4; y = y_hi * 4 + y_lo), z: 8 (z_hi: 2, z_lo: 4; z = z_hi * 4 + z_lo), core: 2. Of those that a mesh axis runs over, the one named last changes fastest.
Arguments:
- slope_up: float32 [128, 768, 3072], P(('ens', 'replica'), None, 'model'), parts along dimension 0, may hold values from -1.25 to 1.25
- slope_down: float32 [128, 3072, 768], P(('ens', 'replica'), 'model'), parts along dimension 0, may hold values from -1.25 to 1.25
- slope_norm: float32 [128, 768], P(('ens', 'replica')), parts along dimension 0, may hold values from -12 to 12
- slope_bias: float32 [128, 768], P(('ens', 'replica')), parts along dimension 0, may hold values from -12 to 12
- param_up: float32 [3072, 3072], P(('ens', 'replica'), 'model'), parts along dimension 0, may hold values from -0.4375 to 0.4375
- param_down: float32 [12288, 768], P(('ens', 'model'), 'replica'), parts along dimension 0, may hold values from -0.21875 to 0.21875
- param_norm: float32 [3072], P(('ens', 'replica')), parts along dimension 0, may hold values from 0.25 to 1.75
- param_bias: float32 [3072], P(('ens', 'replica')), parts along dimension 0, may hold values from -3 to 3
Outputs:
- half_up: bfloat16 [3072, 3072], P('ens', 'model'), parts along dimension 0
- half_down: bfloat16 [12288, 768], P(('ens', 'model')), parts along dimension 0
- half_norm: bfloat16 [3072], P('ens'), parts along dimension 0
- half_bias: bfloat16 [3072], P('ens'), parts along dimension 0
- next_up: float32 [3072, 3072], P(('ens', 'replica'), 'model'), parts along dimension 0
- next_down: float32 [12288, 768], P(('ens', 'model'), 'replica'), parts along dimension 0
- next_norm: float32 [3072], P(('ens', 'replica')), parts along dimension 0
- next_bias: float32 [3072], P(('ens', 'replica')), parts along dimension 0
There are 4 independent parts, one for each index of `ens`. A program takes and returns all parts, laid end to end along the dimension named above; each array names one. Nothing has to cross between parts.
All inputs are finite; a program needn't handle non-finite values.
Results may differ from a plain program's by a relative error of at most 0.0004.
Values may be sent and summed in bfloat16 or wider, within the bound.
No kernel may reach another device: no remote copies, remote signals or barrier semaphores. Data moves between devices by JAX's collectives and lax.ppermute only.
A program may use at most 64 MiB of HBM per device.

v0:
```python
import jax
import jax.numpy as jnp
from jax import lax
from jax.sharding import Mesh
from jax.sharding import PartitionSpec as P

REPLICA = ("replica_0", "replica_1", "replica_2")
ENS_REPLICA = ("ens", "replica_0", "replica_1", "replica_2")
learn_rate = 0.4


def split_up(shard, dim, count):
    lengths = shard.shape
    tiles = shard.reshape(*lengths[:dim], count, lengths[dim] // count, *lengths[dim + 1 :])
    return jnp.moveaxis(tiles, dim, 0)


def sum_at_owner(shard, axis, dim):
    count = lax.axis_size(axis)
    tiles = lax.all_to_all(split_up(shard, dim, count), axis, 0, 0, tiled=True)
    return jnp.sum(tiles, axis=0)


def sum_by_axis(shard, axes, dim):
    far, near = axes
    tiles = split_up(shard, dim, lax.axis_size(far))
    nearer = sum_at_owner(tiles, near, dim + 1)
    arrived = lax.all_to_all(nearer, far, split_axis=0, concat_axis=0, tiled=True)
    return arrived.sum(axis=0)


def from_everyone(shard, axis):
    count = lax.axis_size(axis)
    return lax.all_to_all(
        jnp.broadcast_to(shard[None], (count, *shard.shape)), axis, 0, 0, tiled=True
    )


def taken_together(shard, axis):
    return from_everyone(shard, axis).sum(axis=0)


def together(arrays, axis):
    ends = [0]
    for a in arrays:
        ends.append(ends[-1] + a.size)
    total = taken_together(jnp.concatenate([a.ravel() for a in arrays]), axis)
    return tuple((total[b:e].reshape(a.shape) for a, b, e in zip(arrays, ends, ends[1:])))


def gather_turned(arrays, axis, dims):
    turned = [jnp.moveaxis(a, dim, 0) for a, dim in zip(arrays, dims)]
    both = jnp.concatenate([t.reshape(len(t), -1) for t in turned], axis=1)
    whole, at, outs = (lax.all_gather(both, axis, axis=0, tiled=True), 0, [])
    for t, dim in zip(turned, dims):
        section = whole[:, at : at + t[0].size].reshape(-1, *t.shape[1:])
        outs.append(jnp.moveaxis(section, 0, dim))
        at += t[0].size
    return tuple(outs)


def on_device(
    slope_up, slope_down, slope_norm, slope_bias, param_up, param_down, param_norm, param_bias
):
    mean_up, mean_down, mean_norm, mean_bias = (
        sum_by_axis(slope_up[0], (("replica_0", "replica_1"), "replica_2"), 0),
        sum_by_axis(slope_down[0], (("replica_0", "replica_1"), "replica_2"), 1),
        sum_by_axis(slope_norm[0], (("replica_0", "replica_1"), "replica_2"), 0),
        sum_by_axis(slope_bias[0], (("replica_0", "replica_1"), "replica_2"), 0),
    )
    mean_rate = lax.axis_size(REPLICA) ** (-0.5)
    mean_up = mean_up * mean_rate
    mean_down = mean_down * mean_rate
    mean_norm = mean_norm * mean_rate
    mean_bias = mean_bias * mean_rate
    own_up, own_down, slope_up_norm, slope_down_norm = together(
        (
            jnp.sum(param_up * param_up, axis=1, keepdims=True),
            jnp.sum(param_down * param_down, axis=0, keepdims=True),
            jnp.sum(mean_up * mean_up, axis=1, keepdims=True),
            jnp.sum(mean_down * mean_down, axis=0, keepdims=True),
        ),
        "model",
    )
    mean_up = mean_up * (jnp.sqrt(own_up) * lax.rsqrt(slope_up_norm + 1e-06))
    mean_down = mean_down * (jnp.sqrt(own_down) * lax.rsqrt(slope_down_norm + 1e-06))
    next_up = param_up - learn_rate * mean_up
    next_down = param_down - learn_rate * mean_down
    next_norm = param_norm - learn_rate * mean_norm
    next_bias = param_bias - learn_rate * mean_bias
    half_up, half_down, half_norm, half_bias = gather_turned(
        (
            next_up.astype(jnp.bfloat16),
            next_down.astype(jnp.bfloat16),
            next_norm.astype(jnp.bfloat16),
            next_bias.astype(jnp.bfloat16),
        ),
        REPLICA,
        (0, 1, 0, 0),
    )
    return (half_up, half_down, half_norm, half_bias, next_up, next_down, next_norm, next_bias)


def solution(mesh):
    split = Mesh(
        mesh.devices.reshape(mesh.shape["ens"], 4, 4, 2, mesh.shape["model"]),
        ("ens", "replica_0", "replica_1", "replica_2", "model"),
    )
    placed = (
        P(ENS_REPLICA, None, "model"),
        P(ENS_REPLICA, "model", None),
        P(ENS_REPLICA, None),
        P(ENS_REPLICA, None),
        P(ENS_REPLICA, "model"),
        P(("ens", "model"), REPLICA),
        P(ENS_REPLICA),
        P(ENS_REPLICA),
    )
    return jax.shard_map(
        on_device,
        mesh=split,
        in_specs=placed,
        out_specs=(
            P("ens", "model"),
            P(("ens", "model"), None),
            P("ens"),
            P("ens"),
            P(ENS_REPLICA, "model"),
            P(("ens", "model"), REPLICA),
            P(ENS_REPLICA),
            P(ENS_REPLICA),
        ),
        check_vma=False,
    )
```

profile of v0, /device:TPU:1, one launch (start us, length us, event | category | flops | bytes accessed | tf_op | source)
XLA Modules:
  0.0 228.4 jit_solution(1284755570534542590)
XLA Ops:
  7.2 0.7 reduce.3
  7.9 0.1 reshape_reshape_squeeze.10
  8.0 0.7 reshape.64
  8.6 10.0 %all-to-all-start.5 = ((f32[2,1,384]{2,1,0:T(1,128)}), f32[2,1,384]{2,1,0:T(1,128)S(1)}, u32[]{:S(2)}, u32[]{:S(2)}) async-start(f32[2,1,384]{2,1,0:T(1,128)} %reshape.64), calls=%async_computation.5 | async-start | bytes 6144 | tf_op jit(solution)/shard_map/all_to_all | solution.py:20
  18.7 0.7 reduce.4
  19.4 0.1 reshape_reshape_squeeze.11
  19.5 0.7 reshape.66
  20.2 3.2 %all-to-all-start.7 = ((f32[2,1,384]{2,1,0:T(1,128)}), f32[2,1,384]{2,1,0:T(1,128)S(1)}, u32[]{:S(2)}, u32[]{:S(2)}) async-start(f32[2,1,384]{2,1,0:T(1,128)} %reshape.66), calls=%async_computation.7 | async-start | bytes 6144 | tf_op jit(solution)/shard_map/all_to_all | solution.py:20
  23.4 0.5 broadcast.24
  23.9 0.7 reduce.9
  24.6 0.1 reshape.65
  24.7 1.8 copy.47
  26.5 3.0 %copy.48 = f32[1,768,768]{1,2,0:T(8,128)} copy(f32[1,768,768]{2,1,0:T(8,128)} %param.9) | data formatting | bytes 4718592 | tf_op args[1]
  29.6 3.3 %copy.49 = f32[2,16,768,24]{2,3,1,0:T(8,128)} copy(f32[2,16,768,24]{2,3,0,1:T(8,128)} %bitcast.23) | data formatting | bytes 4718592 | tf_op jit(solution)/shard_map/transpose | solution.py:15
  32.8 0.6 reduce_sum.126
  33.4 6.3 %all_to_all.54 = f32[2,16,24,768]{3,2,1,0:T(8,128)} all-to-all(f32[2,16,24,768]{3,2,1,0:T(8,128)S(1)} %copy.47), channel_id=1, replica_groups=mesh['ens'=4,'replica_0'=4,'replica_1'=4,'replica_2'=2,'model'=4] {'repl..., dimensions={0} | all-to-all | bytes 4718592 | tf_op jit(solution)/shard_map/all_to_all | solution.py:20
  39.7 5.6 %all_to_all.55 = f32[2,16,768,24]{2,3,1,0:T(8,128)S(1)} all-to-all(f32[2,16,768,24]{2,3,1,0:T(8,128)S(1)} %copy-done), channel_id=1, replica_groups=mesh['ens'=4,'replica_0'=4,'replica_1'=4,'replica_2'=2,'model'=4] {'repl..., dimensions={0} | all-to-all | bytes 4718592 | tf_op jit(solution)/shard_map/all_to_all | solution.py:20
  45.4 3.5 %all-to-all-start.6 = ((f32[16,1,24]{2,1,0:T(1,128)}), f32[16,1,24]{2,1,0:T(1,128)S(1)}, u32[]{:S(2)}, u32[]{:S(2)}) async-start(f32[16,1,24]{2,1,0:T(1,128)} %bitcast.9), calls=%async_computation.6 | async-start | bytes 16384 | tf_op jit(solution)/shard_map/all_to_all | solution.py:28
  48.8 0.7 reduce.10
  49.5 0.1 reshape.67
  49.6 0.6 reduce_sum.128
  50.2 5.3 %all-to-all-done.6 = f32[16,1,24]{2,1,0:T(1,128)S(1)} async-done(((f32[16,1,24]{2,1,0:T(1,128)}), f32[16,1,24]{2,1,0:T(1,128)S(1)}, u32[]{:S(2)}, u32[]{:S(2)}) %all-to-all-start.6) | async-done | bytes 1568 | tf_op jit(solution)/shard_map/all_to_all | solution.py:28
  55.5 3.5 %all-to-all-start.8 = ((f32[16,1,24]{2,1,0:T(1,128)}), f32[16,1,24]{2,1,0:T(1,128)S(1)}, u32[]{:S(2)}, u32[]{:S(2)}) async-start(f32[16,1,24]{2,1,0:T(1,128)} %bitcast.12), calls=%async_computation.8 | async-start | bytes 16384 | tf_op jit(solution)/shard_map/all_to_all | solution.py:28
  59.0 3.0 %reduce_sum.117 = f32[16,24,768]{2,1,0:T(8,128)} reduce(f32[2,16,24,768]{3,2,1,0:T(8,128)} %all_to_all.54, f32[]{:T(128)} %constant.5.clone.1), dimensions={0}, to_apply=%region_0.0 | reduce | flops 294912 | bytes 3538948 | tf_op jit(solution)/shard_map/reduce_sum | solution.py:21
  61.9 3.7 %all-to-all-done.8 = f32[16,1,24]{2,1,0:T(1,128)S(1)} async-done(((f32[16,1,24]{2,1,0:T(1,128)}), f32[16,1,24]{2,1,0:T(1,128)S(1)}, u32[]{:S(2)}, u32[]{:S(2)}) %all-to-all-start.8) | async-done | bytes 1568 | tf_op jit(solution)/shard_map/all_to_all | solution.py:28
  65.7 3.7 %all-to-all-start.1 = ((f32[16,24,768]{2,1,0:T(8,128)}), f32[16,24,768]{2,1,0:T(8,128)S(1)}, u32[]{:S(2)}, u32[]{:S(2)}) async-start(f32[16,24,768]{2,1,0:T(8,128)} %reduce_sum.117), calls=%async_computation.1 | async-start | bytes 2359296 | tf_op jit(solution)/shard_map/all_to_all | solution.py:28
  69.4 1.3 reduce_sum.122
  70.7 23.0 %all-to-all-done.1 = f32[16,24,768]{2,1,0:T(8,128)S(1)} async-done(((f32[16,24,768]{2,1,0:T(8,128)}), f32[16,24,768]{2,1,0:T(8,128)S(1)}, u32[]{:S(2)}, u32[]{:S(2)}) %all-to-all-start.1) | async-done | bytes 1179680 | tf_op jit(solution)/shard_map/all_to_all | solution.py:28
  93.7 8.4 %all-to-all-start.3 = ((f32[16,768,24]{1,2,0:T(8,128)}), f32[16,768,24]{1,2,0:T(8,128)S(1)}, u32[]{:S(2)}, u32[]{:S(2)}) async-start(f32[16,768,24]{1,2,0:T(8,128)} %reduce_sum.122), calls=%async_computation.3 | async-start | bytes 2359296 | tf_op jit(solution)/shard_map/all_to_all | solution.py:28
  102.1 0.1 multiply_reduce_fusion.3
  102.2 0.1 multiply_reduce_fusion.2
  102.4 0.5 convert_bitcast_fusion.2
  103.0 0.1 multiply_reduce_fusion.1
  103.1 23.3 %all-to-all-done.3 = f32[16,768,24]{1,2,0:T(8,128)S(1)} async-done(((f32[16,768,24]{1,2,0:T(8,128)}), f32[16,768,24]{1,2,0:T(8,128)S(1)}, u32[]{:S(2)}, u32[]{:S(2)}) %all-to-all-start.3) | async-done | bytes 1179680 | tf_op jit(solution)/shard_map/all_to_all | solution.py:28
  126.5 0.1 multiply_reduce_fusion
  126.7 0.6 broadcast_in_dim.2
  127.3 10.9 %all-to-all-start.4 = ((f32[4,1,96]{2,1,0:T(1,128)}), f32[4,1,96]{2,1,0:T(1,128)S(1)}, u32[]{:S(2)}, u32[]{:S(2)}) async-start(f32[4,1,96]{2,1,0:T(1,128)} %broadcast_in_dim.2), calls=%async_computation.4 | async-start | bytes 4096 | tf_op jit(solution)/shard_map/all_to_all | solution.py:34
  138.2 0.5 convert_bitcast_fusion.1
  138.7 0.1 copy.54
  138.8 0.1 copy.55
  138.9 10.6 %all-to-all-done.4 = f32[4,1,96]{2,1,0:T(1,128)S(1)} async-done(((f32[4,1,96]{2,1,0:T(1,128)}), f32[4,1,96]{2,1,0:T(1,128)S(1)}, u32[]{:S(2)}, u32[]{:S(2)}) %all-to-all-start.4) | async-done | bytes 1568 | tf_op jit(solution)/shard_map/all_to_all | solution.py:34
  149.6 0.7 convert_bitcast_fusion
  150.3 0.7 fusion
  151.0 0.7 concatenate.7
  151.8 63.6 %all-gather.2.cloned.1.call-done = bf16[768,1538]{1,0:T(8,128)(2,1)} async-done(((bf16[24,1538]{1,0:T(8,128)(2,1)}), bf16[768,1538]{1,0:T(8,128)(2,1)}) %all-gather.2.cloned.1.call-update) | async-done | bytes 2362384 | tf_op jit(solution)/shard_map/all_gather | solution.py:54
  215.4 2.8 %slice_bitcast_fusion = (bf16[768,768]{0,1:T(8,128)(2,1)S(1)}, bf16[768,768]{1,0:T(8,128)(2,1)}) fusion(bf16[768,1538]{1,0:T(8,128)(2,1)} %all-gather.2.cloned.1.call-done), kind=kLoop, calls=%fused_computation | loop fusion | bytes 4718592 | tf_op jit(solution)/shard_map/transpose | solution.py:57
  218.2 1.4 copy.56
  219.6 1.9 slice_reduce_fusion
  (23 shorter events, 0.4 us)
Async XLA Ops:
  8.6 11.5 %all-to-all-start.5 = ((f32[2,1,384]{2,1,0:T(1,128)}), f32[2,1,384]{2,1,0:T(1,128)S(1)}, u32[]{:S(2)}, u32[]{:S(2)}) async-start(f32[2,1,384]{2,1,0:T(1,128)} %reshape.64), calls=%async_computation.5 | async-start | bytes 6144 | tf_op jit(solution)/shard_map/all_to_all | solution.py:20
  20.2 13.3 %all-to-all-start.7 = ((f32[2,1,384]{2,1,0:T(1,128)}), f32[2,1,384]{2,1,0:T(1,128)S(1)}, u32[]{:S(2)}, u32[]{:S(2)}) async-start(f32[2,1,384]{2,1,0:T(1,128)} %reshape.66), calls=%async_computation.7 | async-start | bytes 6144 | tf_op jit(solution)/shard_map/all_to_all | solution.py:20
  33.4 6.3 %copy-start = (f32[2,16,768,24]{2,3,1,0:T(8,128)S(1)}, f32[2,16,768,24]{2,3,1,0:T(8,128)}, u32[]{:S(2)}) copy-start(f32[2,16,768,24]{2,3,1,0:T(8,128)} %copy.49) | copy-start | bytes 7077892
  45.4 10.2 %all-to-all-start.6 = ((f32[16,1,24]{2,1,0:T(1,128)}), f32[16,1,24]{2,1,0:T(1,128)S(1)}, u32[]{:S(2)}, u32[]{:S(2)}) async-start(f32[16,1,24]{2,1,0:T(1,128)} %bitcast.9), calls=%async_computation.6 | async-start | bytes 16384 | tf_op jit(solution)/shard_map/all_to_all | solution.py:28
  55.5 10.2 %all-to-all-start.8 = ((f32[16,1,24]{2,1,0:T(1,128)}), f32[16,1,24]{2,1,0:T(1,128)S(1)}, u32[]{:S(2)}, u32[]{:S(2)}) async-start(f32[16,1,24]{2,1,0:T(1,128)} %bitcast.12), calls=%async_computation.8 | async-start | bytes 16384 | tf_op jit(solution)/shard_map/all_to_all | solution.py:28
  65.7 28.0 %all-to-all-start.1 = ((f32[16,24,768]{2,1,0:T(8,128)}), f32[16,24,768]{2,1,0:T(8,128)S(1)}, u32[]{:S(2)}, u32[]{:S(2)}) async-start(f32[16,24,768]{2,1,0:T(8,128)} %reduce_sum.117), calls=%async_computation.1 | async-start | bytes 2359296 | tf_op jit(solution)/shard_map/all_to_all | solution.py:28
  70.6 31.4 %copy-start.2 = (f32[24,768]{1,0:T(8,128)S(1)}, f32[24,768]{1,0:T(8,128)}, u32[]{:S(2)}) copy-start(f32[24,768]{1,0:T(8,128)} %param.12) | copy-start | bytes 221188
  70.6 31.5 %copy-start.1 = (f32[768,24]{0,1:T(8,128)S(1)}, f32[768,24]{0,1:T(8,128)}, u32[]{:S(2)}) copy-start(f32[768,24]{0,1:T(8,128)} %param.13) | copy-start | bytes 221188
  70.7 31.7 %copy-start.3 = (f32[24]{0:T(128)S(1)}, f32[24]{0:T(128)}, u32[]{:S(2)}) copy-start(f32[24]{0:T(128)} %param.14) | copy-start | bytes 292
  70.7 67.6 %copy-start.4 = (f32[24]{0:T(128)S(1)}, f32[24]{0:T(128)}, u32[]{:S(2)}) copy-start(f32[24]{0:T(128)} %param.15) | copy-start | bytes 292
  93.7 32.8 %all-to-all-start.3 = ((f32[16,768,24]{1,2,0:T(8,128)}), f32[16,768,24]{1,2,0:T(8,128)S(1)}, u32[]{:S(2)}, u32[]{:S(2)}) async-start(f32[16,768,24]{1,2,0:T(8,128)} %reduce_sum.122), calls=%async_computation.3 | async-start | bytes 2359296 | tf_op jit(solution)/shard_map/all_to_all | solution.py:28
  127.3 22.2 %all-to-all-start.4 = ((f32[4,1,96]{2,1,0:T(1,128)}), f32[4,1,96]{2,1,0:T(1,128)S(1)}, u32[]{:S(2)}, u32[]{:S(2)}) async-start(f32[4,1,96]{2,1,0:T(1,128)} %broadcast_in_dim.2), calls=%async_computation.4 | async-start | bytes 4096 | tf_op jit(solution)/shard_map/all_to_all | solution.py:34
  138.2 77.2 %all-gather.2.cloned.1.call-start = ((), (), s32[]{:S(2)}) async-start(), calls=%async_computation.9 | async-start | bytes 2635776 | tf_op jit(solution)/shard_map/all_gather | solution.py:54
Sparse Core Ops, SparseCore 0:
  151.9 63.4 all-gather.1
where the time goes:
time: 229 us; the launch traced here: 228 us
  waiting for transfers between devices  130 us (57%)
  starting transfers between devices  43.3 us (19%)
  local copies, waits for them, and re-layouts  18 us (8%)
  between operations  14.2 us (6%)
  blocking collectives  11.9 us (5%)
  other arithmetic  11.5 us (5%)
    all_gather x1, waiting for transfers between devices, gather_turned(): whole, at, outs = (lax.all_gather(both, axis, axis=0, tiled=True), 0, [])  63.6 us
    all_to_all x4, waiting for transfers between devices, sum_by_axis(): lax.all_to_all(nearer, far, split_axis=0, concat_axis=0, tiled=True)  55.4 us
    all_to_all x4, starting transfers between devices, sum_by_axis(): lax.all_to_all(nearer, far, split_axis=0, concat_axis=0, tiled=True)  19 us
    all_to_all x2, starting transfers between devices, sum_at_owner(): tiles = lax.all_to_all(split_up(shard, dim, count), axis, 0, 0, tiled=True)  13.3 us
    all_to_all x2, blocking collectives, sum_at_owner(): tiles = lax.all_to_all(split_up(shard, dim, count), axis, 0, 0, tiled=True)  11.9 us
    all_to_all x1, starting transfers between devices, from_everyone(): lax.all_to_all(jnp.broadcast_to(shard[None], (count, *shard.shape)), axis...  10.9 us
    all_to_all x1, waiting for transfers between devices, from_everyone(): lax.all_to_all(jnp.broadcast_to(shard[None], (count, *shard.shape)), axis...  10.6 us
    unnamed x16, local copies, waits for them, and re-layouts  6 us
  transfers between devices with their start and end apart: 8, of which 6 were waited for; matrix products, arithmetic and copies ran while one was open for 8% of the time, Pallas kernels for 0%

commit v1 on v0

--- a/solution.py
+++ b/solution.py
@@ -7,6 +7,12 @@
 REPLICA = ("replica_0", "replica_1", "replica_2")
 ENS_REPLICA = ("ens", "replica_0", "replica_1", "replica_2")
 learn_rate = 0.4
+
+
+def shifts_all_get(work_x, which_axis):
+    field_out = jnp.stack([work_x for _ in range(jax.lax.psum(1, which_axis))], axis=0)
+    base_arr = jax.lax.all_to_all(field_out, which_axis, 0, 0)
+    return jnp.concatenate(base_arr, axis=0)
 
 
 def split_up(shard, dim, count):
@@ -51,7 +57,7 @@
 def gather_turned(arrays, axis, dims):
     turned = [jnp.moveaxis(a, dim, 0) for a, dim in zip(arrays, dims)]
     both = jnp.concatenate([t.reshape(len(t), -1) for t in turned], axis=1)
-    whole, at, outs = (lax.all_gather(both, axis, axis=0, tiled=True), 0, [])
+    whole, at, outs = (shifts_all_get(both, which_axis=axis), 0, [])
     for t, dim in zip(turned, dims):
         section = whole[:, at : at + t[0].size].reshape(-1, *t.shape[1:])
         outs.append(jnp.moveaxis(section, 0, dim))

time: 229 us -> 221 us (0.965)
  blocking collectives: 11.9 us -> 83.5 us
  waiting for transfers between devices: 130 us -> 65.9 us
  between operations: 14.2 us -> 0.77 us
  local copies, waits for them, and re-layouts: 18 us -> 14.9 us
    all_to_all x0 -> x1, blocking collectives: none -> 71.6 us  [shifts_all_get(): base_arr = jax.lax.all_to_all(field_out, which_axis, 0, 0)]
    all_gather x1 -> x0, waiting for transfers between devices: 63.6 us -> none  [gather_turned(): whole, at, outs = (lax.all_gather(both, axis, axis=0, tiled=True), 0, [])]
  transfers between devices with their start and end apart: 8 -> 7, of which waited for: 6 -> 5; matrix products, arithmetic and copies ran while one was open for 8% -> 9% of each run, Pallas kernels for 0% -> 0%
where the time goes in v1:
time: 221 us; the launch traced here: 220 us
  blocking collectives  83.5 us (38%)
  waiting for transfers between devices  65.9 us (30%)
  starting transfers between devices  43.3 us (20%)
  local copies, waits for them, and re-layouts  14.9 us (7%)
  other arithmetic  11.5 us (5%)
    all_to_all x1, blocking collectives, shifts_all_get(): base_arr = jax.lax.all_to_all(field_out, which_axis, 0, 0)  71.6 us
    all_to_all x4, waiting for transfers between devices, sum_by_axis(): lax.all_to_all(nearer, far, split_axis=0, concat_axis=0, tiled=True)  55.4 us
    all_to_all x4, starting transfers between devices, sum_by_axis(): lax.all_to_all(nearer, far, split_axis=0, concat_axis=0, tiled=True)  19 us
    all_to_all x2, starting transfers between devices, sum_at_owner(): tiles = lax.all_to_all(split_up(shard, dim, count), axis, 0, 0, tiled=True)  13.3 us
    all_to_all x2, blocking collectives, sum_at_owner(): tiles = lax.all_to_all(split_up(shard, dim, count), axis, 0, 0, tiled=True)  11.9 us
    all_to_all x1, starting transfers between devices, from_everyone(): lax.all_to_all(jnp.broadcast_to(shard[None], (count, *shard.shape)), axis...  10.9 us
    all_to_all x1, waiting for transfers between devices, from_everyone(): lax.all_to_all(jnp.broadcast_to(shard[None], (count, *shard.shape)), axis...  10.6 us
    unnamed x16, local copies, waits for them, and re-layouts  6 us
  transfers between devices with their start and end apart: 7, of which 5 were waited for; matrix products, arithmetic and copies ran while one was open for 9% of the time, Pallas kernels for 0%

profile of v1, /device:TPU:1, one launch (start us, length us, event | category | flops | bytes accessed | tf_op | source)
XLA Modules:
  0.0 219.8 jit_solution(13088483646720810155)
XLA Ops:
  0.6 0.7 reduce.3
  1.3 0.1 reshape_reshape_squeeze.10
  1.4 0.7 reshape.70
  2.1 10.0 %all-to-all-start.5 = ((f32[2,1,384]{2,1,0:T(1,128)}), f32[2,1,384]{2,1,0:T(1,128)S(1)}, u32[]{:S(2)}, u32[]{:S(2)}) async-start(f32[2,1,384]{2,1,0:T(1,128)} %reshape.70), calls=%async_computation.5 | async-start | bytes 6144 | tf_op jit(solution)/shard_map/all_to_all | solution.py:26
  12.2 0.7 reduce.4
  12.9 0.1 reshape_reshape_squeeze.11
  13.0 0.7 reshape.72
  13.6 3.2 %all-to-all-start.7 = ((f32[2,1,384]{2,1,0:T(1,128)}), f32[2,1,384]{2,1,0:T(1,128)S(1)}, u32[]{:S(2)}, u32[]{:S(2)}) async-start(f32[2,1,384]{2,1,0:T(1,128)} %reshape.72), calls=%async_computation.7 | async-start | bytes 6144 | tf_op jit(solution)/shard_map/all_to_all | solution.py:26
  16.9 0.5 broadcast.26
  17.4 0.7 reduce.9
  18.0 0.1 reshape.71
  18.1 1.8 copy.52
  20.0 3.0 %copy.53 = f32[1,768,768]{1,2,0:T(8,128)} copy(f32[1,768,768]{2,1,0:T(8,128)} %param.9) | data formatting | bytes 4718592 | tf_op args[1]
  23.0 3.3 %copy.54 = f32[2,16,768,24]{2,3,1,0:T(8,128)} copy(f32[2,16,768,24]{2,3,0,1:T(8,128)} %bitcast.26) | data formatting | bytes 4718592 | tf_op jit(solution)/shard_map/transpose | solution.py:21
  26.3 0.6 reduce_sum.126
  26.9 6.3 %all_to_all.59 = f32[2,16,24,768]{3,2,1,0:T(8,128)} all-to-all(f32[2,16,24,768]{3,2,1,0:T(8,128)S(1)} %copy.52), channel_id=1, replica_groups=mesh['ens'=4,'replica_0'=4,'replica_1'=4,'replica_2'=2,'model'=4] {'repl..., dimensions={0} | all-to-all | bytes 4718592 | tf_op jit(solution)/shard_map/all_to_all | solution.py:26
  33.2 5.6 %all_to_all.60 = f32[2,16,768,24]{2,3,1,0:T(8,128)S(1)} all-to-all(f32[2,16,768,24]{2,3,1,0:T(8,128)S(1)} %copy-done), channel_id=1, replica_groups=mesh['ens'=4,'replica_0'=4,'replica_1'=4,'replica_2'=2,'model'=4] {'repl..., dimensions={0} | all-to-all | bytes 4718592 | tf_op jit(solution)/shard_map/all_to_all | solution.py:26
  38.8 3.5 %all-to-all-start.6 = ((f32[16,1,24]{2,1,0:T(1,128)}), f32[16,1,24]{2,1,0:T(1,128)S(1)}, u32[]{:S(2)}, u32[]{:S(2)}) async-start(f32[16,1,24]{2,1,0:T(1,128)} %bitcast.9), calls=%async_computation.6 | async-start | bytes 16384 | tf_op jit(solution)/shard_map/all_to_all | solution.py:34
  42.3 0.7 reduce.10
  43.1 0.6 reduce_sum.128
  43.7 5.3 %all-to-all-done.6 = f32[16,1,24]{2,1,0:T(1,128)S(1)} async-done(((f32[16,1,24]{2,1,0:T(1,128)}), f32[16,1,24]{2,1,0:T(1,128)S(1)}, u32[]{:S(2)}, u32[]{:S(2)}) %all-to-all-start.6) | async-done | bytes 1568 | tf_op jit(solution)/shard_map/all_to_all | solution.py:34
  49.0 3.5 %all-to-all-start.8 = ((f32[16,1,24]{2,1,0:T(1,128)}), f32[16,1,24]{2,1,0:T(1,128)S(1)}, u32[]{:S(2)}, u32[]{:S(2)}) async-start(f32[16,1,24]{2,1,0:T(1,128)} %bitcast.12), calls=%async_computation.8 | async-start | bytes 16384 | tf_op jit(solution)/shard_map/all_to_all | solution.py:34
  52.5 3.0 %reduce_sum.117 = f32[16,24,768]{2,1,0:T(8,128)} reduce(f32[2,16,24,768]{3,2,1,0:T(8,128)} %all_to_all.59, f32[]{:T(128)} %constant.5.clone.1), dimensions={0}, to_apply=%region_0.0 | reduce | flops 294912 | bytes 3538948 | tf_op jit(solution)/shard_map/reduce_sum | solution.py:27
  55.4 3.7 %all-to-all-done.8 = f32[16,1,24]{2,1,0:T(1,128)S(1)} async-done(((f32[16,1,24]{2,1,0:T(1,128)}), f32[16,1,24]{2,1,0:T(1,128)S(1)}, u32[]{:S(2)}, u32[]{:S(2)}) %all-to-all-start.8) | async-done | bytes 1568 | tf_op jit(solution)/shard_map/all_to_all | solution.py:34
  59.1 3.7 %all-to-all-start.1 = ((f32[16,24,768]{2,1,0:T(8,128)}), f32[16,24,768]{2,1,0:T(8,128)S(1)}, u32[]{:S(2)}, u32[]{:S(2)}) async-start(f32[16,24,768]{2,1,0:T(8,128)} %reduce_sum.117), calls=%async_computation.1 | async-start | bytes 2359296 | tf_op jit(solution)/shard_map/all_to_all | solution.py:34
  62.8 1.3 reduce_sum.122
  64.1 23.0 %all-to-all-done.1 = f32[16,24,768]{2,1,0:T(8,128)S(1)} async-done(((f32[16,24,768]{2,1,0:T(8,128)}), f32[16,24,768]{2,1,0:T(8,128)S(1)}, u32[]{:S(2)}, u32[]{:S(2)}) %all-to-all-start.1) | async-done | bytes 1179680 | tf_op jit(solution)/shard_map/all_to_all | solution.py:34
  87.1 8.4 %all-to-all-start.3 = ((f32[16,768,24]{1,2,0:T(8,128)}), f32[16,768,24]{1,2,0:T(8,128)S(1)}, u32[]{:S(2)}, u32[]{:S(2)}) async-start(f32[16,768,24]{1,2,0:T(8,128)} %reduce_sum.122), calls=%async_computation.3 | async-start | bytes 2359296 | tf_op jit(solution)/shard_map/all_to_all | solution.py:34
  95.5 0.1 multiply_reduce_fusion.3
  95.7 0.1 multiply_reduce_fusion.2
  95.8 0.5 convert_bitcast_fusion.2
  96.4 0.1 multiply_reduce_fusion.1
  96.6 23.3 %all-to-all-done.3 = f32[16,768,24]{1,2,0:T(8,128)S(1)} async-done(((f32[16,768,24]{1,2,0:T(8,128)}), f32[16,768,24]{1,2,0:T(8,128)S(1)}, u32[]{:S(2)}, u32[]{:S(2)}) %all-to-all-start.3) | async-done | bytes 1179680 | tf_op jit(solution)/shard_map/all_to_all | solution.py:34
  120.0 0.1 multiply_reduce_fusion
  120.2 0.6 broadcast_in_dim.2
  120.7 10.9 %all-to-all-start.4 = ((f32[4,1,96]{2,1,0:T(1,128)}), f32[4,1,96]{2,1,0:T(1,128)S(1)}, u32[]{:S(2)}, u32[]{:S(2)}) async-start(f32[4,1,96]{2,1,0:T(1,128)} %broadcast_in_dim.2), calls=%async_computation.4 | async-start | bytes 4096 | tf_op jit(solution)/shard_map/all_to_all | solution.py:40
  131.7 0.5 convert_bitcast_fusion.1
  132.2 0.1 copy.59
  132.3 0.1 copy.60
  132.4 10.6 %all-to-all-done.4 = f32[4,1,96]{2,1,0:T(1,128)S(1)} async-done(((f32[4,1,96]{2,1,0:T(1,128)}), f32[4,1,96]{2,1,0:T(1,128)S(1)}, u32[]{:S(2)}, u32[]{:S(2)}) %all-to-all-start.4) | async-done | bytes 1568 | tf_op jit(solution)/shard_map/all_to_all | solution.py:40
  143.1 0.7 convert_bitcast_fusion
  143.8 0.7 fusion
  144.5 0.1 concatenate.7
  144.6 0.2 stack.2
  144.8 71.6 %all_to_all.61 = bf16[32,24,1538]{2,1,0:T(8,128)(2,1)S(1)} all-to-all(bf16[32,24,1538]{2,1,0:T(8,128)(2,1)S(1)} %stack.2), channel_id=1, replica_groups=mesh['ens'=4,'replica_0'=4,'replica_1'=4,'replica_2'=2,'model'=4] {'repl..., dimensions={0} | all-to-all | bytes 4724736 | tf_op jit(solution)/shard_map/all_to_all | solution.py:14
  216.3 0.9 slice_reduce_fusion
  217.2 1.2 slice_bitcast_fusion
  218.4 1.4 copy.61
  (22 shorter events, 0.5 us)
Async XLA Ops:
  2.1 11.5 %all-to-all-start.5 = ((f32[2,1,384]{2,1,0:T(1,128)}), f32[2,1,384]{2,1,0:T(1,128)S(1)}, u32[]{:S(2)}, u32[]{:S(2)}) async-start(f32[2,1,384]{2,1,0:T(1,128)} %reshape.70), calls=%async_computation.5 | async-start | bytes 6144 | tf_op jit(solution)/shard_map/all_to_all | solution.py:26
  13.6 13.3 %all-to-all-start.7 = ((f32[2,1,384]{2,1,0:T(1,128)}), f32[2,1,384]{2,1,0:T(1,128)S(1)}, u32[]{:S(2)}, u32[]{:S(2)}) async-start(f32[2,1,384]{2,1,0:T(1,128)} %reshape.72), calls=%async_computation.7 | async-start | bytes 6144 | tf_op jit(solution)/shard_map/all_to_all | solution.py:26
  26.9 6.3 %copy-start = (f32[2,16,768,24]{2,3,1,0:T(8,128)S(1)}, f32[2,16,768,24]{2,3,1,0:T(8,128)}, u32[]{:S(2)}) copy-start(f32[2,16,768,24]{2,3,1,0:T(8,128)} %copy.54) | copy-start | bytes 7077892
  38.8 10.2 %all-to-all-start.6 = ((f32[16,1,24]{2,1,0:T(1,128)}), f32[16,1,24]{2,1,0:T(1,128)S(1)}, u32[]{:S(2)}, u32[]{:S(2)}) async-start(f32[16,1,24]{2,1,0:T(1,128)} %bitcast.9), calls=%async_computation.6 | async-start | bytes 16384 | tf_op jit(solution)/shard_map/all_to_all | solution.py:34
  49.0 10.2 %all-to-all-start.8 = ((f32[16,1,24]{2,1,0:T(1,128)}), f32[16,1,24]{2,1,0:T(1,128)S(1)}, u32[]{:S(2)}, u32[]{:S(2)}) async-start(f32[16,1,24]{2,1,0:T(1,128)} %bitcast.12), calls=%async_computation.8 | async-start | bytes 16384 | tf_op jit(solution)/shard_map/all_to_all | solution.py:34
  59.1 28.0 %all-to-all-start.1 = ((f32[16,24,768]{2,1,0:T(8,128)}), f32[16,24,768]{2,1,0:T(8,128)S(1)}, u32[]{:S(2)}, u32[]{:S(2)}) async-start(f32[16,24,768]{2,1,0:T(8,128)} %reduce_sum.117), calls=%async_computation.1 | async-start | bytes 2359296 | tf_op jit(solution)/shard_map/all_to_all | solution.py:34
  64.1 31.4 %copy-start.2 = (f32[24,768]{1,0:T(8,128)S(1)}, f32[24,768]{1,0:T(8,128)}, u32[]{:S(2)}) copy-start(f32[24,768]{1,0:T(8,128)} %param.12) | copy-start | bytes 221188
  64.1 31.5 %copy-start.1 = (f32[768,24]{0,1:T(8,128)S(1)}, f32[768,24]{0,1:T(8,128)}, u32[]{:S(2)}) copy-start(f32[768,24]{0,1:T(8,128)} %param.13) | copy-start | bytes 221188
  64.1 31.7 %copy-start.3 = (f32[24]{0:T(128)S(1)}, f32[24]{0:T(128)}, u32[]{:S(2)}) copy-start(f32[24]{0:T(128)} %param.14) | copy-start | bytes 292
  64.1 67.6 %copy-start.4 = (f32[24]{0:T(128)S(1)}, f32[24]{0:T(128)}, u32[]{:S(2)}) copy-start(f32[24]{0:T(128)} %param.15) | copy-start | bytes 292
  87.1 32.8 %all-to-all-start.3 = ((f32[16,768,24]{1,2,0:T(8,128)}), f32[16,768,24]{1,2,0:T(8,128)S(1)}, u32[]{:S(2)}, u32[]{:S(2)}) async-start(f32[16,768,24]{1,2,0:T(8,128)} %reduce_sum.122), calls=%async_computation.3 | async-start | bytes 2359296 | tf_op jit(solution)/shard_map/all_to_all | solution.py:34
  120.7 22.2 %all-to-all-start.4 = ((f32[4,1,96]{2,1,0:T(1,128)}), f32[4,1,96]{2,1,0:T(1,128)S(1)}, u32[]{:S(2)}, u32[]{:S(2)}) async-start(f32[4,1,96]{2,1,0:T(1,128)} %broadcast_in_dim.2), calls=%async_computation.4 | async-start | bytes 4096 | tf_op jit(solution)/shard_map/all_to_all | solution.py:40
